TPU v7x, 32 devices: a whole 2x2x4 slice. The times are simulated.
32 devices in a mesh: blk: 8 (over y, x, core), uly: 4 (over z).
Axes of the slice: x: 2, y: 2, z: 4, core: 2. Of those that a mesh axis runs over, the one named last changes fastest.
Arguments:
- queries: bfloat16 [4096, 4096], P(('blk', 'uly')), may hold values from -128 to 128
- keys: bfloat16 [4096, 1024], P(('blk', 'uly')), may hold values from -7 to 7
- values: bfloat16 [4096, 1024], P(('blk', 'uly')), may hold values from -6 to 6
- doc_ids: int32 [4096], P(('blk', 'uly')), may hold values from 0 to 31, never falling along the last dimension, each value on 1 to 512 neighbouring positions
- out_weight: bfloat16 [4096, 4096], P('uly'), may hold values from -0.09375 to 0.09375
Outputs:
- mixed: bfloat16 [4096, 4096], P(('blk', 'uly'))
Inputs may be any that keep to these rules, and one draw needn't show every extreme that they name: `doc_ids`: document numbers never fall along the pack; each document holds 1 to 512 consecutive tokens, and some document holds exactly 512.
All inputs are finite; a program needn't handle non-finite values.
Results may differ from a plain program's by a relative error of at most 0.017.
Values may be sent and summed in bfloat16 or wider, within the bound.
A program may use at most 64 MiB of HBM per device.

v0:
```python
import math
import jax
import jax.numpy as jnp
from jax import lax
from jax.sharding import PartitionSpec as P

HEAD_DIM = 128


def shifted(value, axis, steps):
    count = lax.axis_size(axis)
    first, last = (max(0, -steps), min(count, count - steps))
    return lax.ppermute(value, axis, [(source, source + steps) for source in range(first, last)])


def body(queries, keys, values, doc_ids, out_weight):
    n_uly = lax.axis_size("uly")
    blk_index = lax.axis_index("blk")
    rows = queries.shape[0]
    head_dim = HEAD_DIM
    heads = queries.shape[1] // head_dim
    kv_heads = keys.shape[1] // head_dim
    repeat = max(1, n_uly // kv_heads)
    kv_local = max(n_uly, kv_heads) // n_uly
    local_heads = heads // n_uly
    grouped = local_heads // kv_local
    block = rows * n_uly
    sub_rows = math.gcd(block, 512)
    n_sub = block // sub_rows
    scale = 1.0 / math.sqrt(head_dim)
    query_ids = lax.all_gather(doc_ids, "uly", axis=0, tiled=True)
    query_split = queries.reshape(rows, heads, head_dim)
    key_wide = jnp.repeat(keys.reshape(rows, kv_heads, head_dim), repeat, axis=1)
    value_wide = jnp.repeat(values.reshape(rows, kv_heads, head_dim), repeat, axis=1)
    key_wide, value_wide = (key_wide, value_wide)
    query_local, key_local, value_local = (
        lax.all_to_all(query_split, "uly", split_axis=1, concat_axis=0, tiled=True),
        lax.all_to_all(key_wide, "uly", split_axis=1, concat_axis=0, tiled=True),
        lax.all_to_all(value_wide, "uly", split_axis=1, concat_axis=0, tiled=True),
    )
    carried = (key_local, value_local)
    query_grouped = query_local.reshape(n_sub, sub_rows, kv_local, grouped, head_dim)
    query_start = blk_index * block
    query_pos = query_start + jnp.arange(block, dtype=jnp.int32)
    first_id = query_ids[0]
    offsets = jnp.arange(block, dtype=jnp.int32)
    ids_sub = query_ids.reshape(n_sub, sub_rows)
    pos_sub = query_pos.reshape(n_sub, sub_rows)

    def attend(state, pair, key_ids, source):
        key_block, value_block = pair
        key_start = jnp.maximum(source, 0) * block
        key_pos = key_start + offsets
        needed = (source >= 0) & (
            (source == blk_index) | (source < blk_index) & (key_ids[block - 1] == first_id)
        )

        def compute(state_in):

            def one(item):
                query_part, pos_part, ids_part, accum, peak, total = item
                scores = (
                    jnp.einsum(
                        "qkgd,pkd->kgqp", query_part, key_block, preferred_element_type=jnp.float32
                    )
                    * scale
                )
                allowed = (key_pos[None, :] <= pos_part[:, None]) & (
                    key_ids[None, :] == ids_part[:, None]
                )
                scores = jnp.where(allowed, scores, -1e30)
                peak_new = jnp.maximum(peak, jnp.max(scores, axis=-1))
                expo = jnp.where(allowed, jnp.exp(scores - peak_new[..., None]), 0.0)
                factor = jnp.exp(peak - peak_new)
                total_new = total * factor + jnp.sum(expo, axis=-1)
                update = jnp.einsum(
                    "kgqp,pkd->kgqd",
                    expo.astype(jnp.bfloat16),
                    value_block,
                    preferred_element_type=jnp.float32,
                )
                return (accum * factor[..., None] + update, peak_new, total_new)

            return lax.map(
                one, (query_grouped, pos_sub, ids_sub, state_in[0], state_in[1], state_in[2])
            )

        def keep(state_in):
            return state_in

        return lax.cond(needed, compute, keep, state)

    start_state = (
        jnp.zeros((n_sub, kv_local, grouped, sub_rows, head_dim), jnp.float32),
        jnp.full((n_sub, kv_local, grouped, sub_rows), -1e30, jnp.float32),
        jnp.zeros((n_sub, kv_local, grouped, sub_rows), jnp.float32),
    )
    state = attend(start_state, carried, query_ids, blk_index)
    earlier_key, earlier_value, earlier_marks = shifted(
        (carried[0], carried[1], query_ids.astype(jnp.bfloat16)), "blk", 1
    )
    earlier_ids = earlier_marks.astype(jnp.int32)
    state = attend(state, (earlier_key, earlier_value), earlier_ids, blk_index - 1)
    accum, peak, total = state
    attn = (
        (accum / total[..., None])
        .transpose(0, 3, 1, 2, 4)
        .reshape(block, local_heads * head_dim)
        .astype(jnp.bfloat16)
    )
    mixed = lax.psum_scatter(
        jnp.dot(attn, out_weight, preferred_element_type=jnp.float32).astype(jnp.bfloat16),
        "uly",
        scatter_dimension=0,
        tiled=True,
    )
    return mixed


def solution(mesh):
    placed = (
        P(("blk", "uly"), None),
        P(("blk", "uly"), None),
        P(("blk", "uly"), None),
        P(("blk", "uly")),
        P("uly", None),
    )
    return jax.shard_map(
        body, mesh=mesh, in_specs=placed, out_specs=P(("blk", "uly"), None), check_vma=False
    )
```

profile of v0, /device:TPU:0, one launch (start us, length us, event | category | flops | bytes accessed | tf_op | source)
XLA Modules:
  0.0 184.7 jit_solution(14577532152778803910)
XLA Ops:
  6.5 1.8 copy.38
  8.3 6.3 %all-to-all-start.1 = ((bf16[128,8,128]{0,2,1:T(8,128)(2,1)}), bf16[128,8,128]{0,2,1:T(8,128)(2,1)S(1)}, u32[]{:S(2)}, u32[]{:S(2)}) async-start(bf16[128,8,128]{0,2,1:T(8,128)(2,1)} %bitcast.33), calls=%async_computation.1 | async-start | bytes 524288 | tf_op jit(solution)/shard_map/all_to_all | solution.py:38
  14.7 1.8 copy.41
  16.5 7.1 %all-to-all-done.1 = bf16[128,8,128]{0,2,1:T(8,128)(2,1)S(1)} async-done(((bf16[128,8,128]{0,2,1:T(8,128)(2,1)}), bf16[128,8,128]{0,2,1:T(8,128)(2,1)S(1)}, u32[]{:S(2)}, u32[]{:S(2)}) %all-to-all-start.1) | async-done | bytes 262176 | tf_op jit(solution)/shard_map/all_to_all | solution.py:38
  23.6 3.4 %all-to-all-start.2 = ((bf16[128,8,128]{0,2,1:T(8,128)(2,1)}), bf16[128,8,128]{0,2,1:T(8,128)(2,1)S(1)}, u32[]{:S(2)}, u32[]{:S(2)}) async-start(bf16[128,8,128]{0,2,1:T(8,128)(2,1)} %bitcast.38), calls=%async_computation.2 | async-start | bytes 524288 | tf_op jit(solution)/shard_map/all_to_all | solution.py:39
  27.0 1.6 copy.34
  28.6 1.3 copy.35
  29.9 4.1 %all-to-all-done.2 = bf16[128,8,128]{0,2,1:T(8,128)(2,1)S(1)} async-done(((bf16[128,8,128]{0,2,1:T(8,128)(2,1)}), bf16[128,8,128]{0,2,1:T(8,128)(2,1)S(1)}, u32[]{:S(2)}, u32[]{:S(2)}) %all-to-all-start.2) | async-done | bytes 262176 | tf_op jit(solution)/shard_map/all_to_all | solution.py:39
  34.0 3.5 %all-to-all-start = ((bf16[128,32,128]{2,0,1:T(8,128)(2,1)}), bf16[128,32,128]{2,0,1:T(8,128)(2,1)S(1)}, u32[]{:S(2)}, u32[]{:S(2)}) async-start(bf16[128,32,128]{2,0,1:T(8,128)(2,1)} %copy.35), calls=%async_computation | async-start | bytes 2097152 | tf_op jit(solution)/shard_map/all_to_all | solution.py:37
  37.6 0.8 copy.40
  38.4 0.9 copy.43
  39.3 1.3 collective-permute-start.1
  40.6 4.8 %collective-permute-start.2 = (bf16[512,2,128]{2,0,1:T(8,128)(2,1)}, bf16[512,2,128]{2,0,1:T(8,128)(2,1)}, u32[]{:S(2)}, u32[]{:S(2)}) collective-permute-start(bf16[512,2,128]{2,0,1:T(8,128)(2,1)} %bitcast.42), channel_id=1, source_target_pairs={{0,4},{4,8},{8,12},{12,16},{16,20},{20,24},{24,28},{1,5},{5,9},{9,... | collective-permute-start | bytes 786440 | tf_op jit(solution)/shard_map/ppermute | solution.py:13
  45.4 12.3 %all-gather = s32[4,1,128]{2,1,0:T(1,128)S(1)} all-gather(s32[1,1,128]{2,1,0:T(1,128)S(1)} %bitcast.133), channel_id=1, replica_groups=mesh['blk'=8,'uly'=4] {'uly'}, dimensions={0}, use_global_device_ids=true | all-gather | bytes 2560 | tf_op jit(solution)/shard_map/all_gather | solution.py:31
  57.7 1.3 collective-permute-start
  61.8 8.8 %conditional.2 = (f32[1,2,4,512,128]{4,3,2,1,0:T(8,128)S(1)}, f32[1,2,4,512]{3,2,1,0:T(4,128)S(1)}, f32[1,2,4,512]{3,2,1,0:T(4,128)S(1)}) conditional(s32[]{:T(128)} %convert_element_type.35, () %tuple.24, (s32[]{:T(128)}, s32[512]{0:T(512)S(1)}, s32[1,512]{1,0:T(1,128)S(1)}, s32[512]{0:T(512)S(1)}, s32[1,512]{1,0:T(1,128)S(1)}, ...), branch_computations={%region_0.0_spmd, %region_1.4_spmd} | conditional | flops 1102336512 | bytes 30093364 | solution.py:91
  62.1 2.5 %fusion = (f32[2,4,512]{2,1,0:T(4,128)S(1)}, f32[2,512,512,4]{2,1,3,0:T(8,128)S(1)}) fusion(pred[512,512]{0,1:T(8,128)(4,1)S(1)} %compare_and_fusion, bf16[1,512,2,4,128]{4,1,3,2,0:T(8,128)(2,1)S(1)} %get-tuple-element.136, bf16[512,2,128]{2,0,1:T(8,128)(2,1)} %get-tuple-element.134), kind=kOutput, calls=%fused_computation.2 | convolution fusion | flops 543158272 | bytes 9977856 | tf_op jit(solution)/shard_map/cond/branch_1_fun/while/body/eval_jaxpr/qkgd,pkd->kgqp/dot_general | solution.py:63
  64.6 3.9 %add_bitcast_fusion = f32[1,2,4,512,128]{4,3,2,1,0:T(8,128)S(1)} fusion(f32[2,512,512,4]{2,1,3,0:T(8,128)S(1)} %get-tuple-element.172, f32[2,4,512]{2,1,0:T(4,128)S(1)} %get-tuple-element.170, pred[512,512]{0,1:T(8,128)(4,1)S(1)} %compare_and_fusion, f32[2,4,512]{2,1,0:T(4,128)S(1)} %get-tuple-element.169, bf16[512,2,128]{2,0,1:T(8,128)(2,1)} %get-tuple-element.138), kind=kOutput, calls=%fused_computation.7 | convolution fusion | flops 547880960 | bytes 11042816 | tf_op jit(solution)/shard_map/cond/branch_1_fun/while/body/eval_jaxpr/kgqp,pkd->kgqd/dot_general | solution.py:76
  68.5 2.0 %fusion.1 = f32[2,4,512]{2,1,0:T(4,128)S(1)} fusion(f32[2,512,512,4]{2,1,3,0:T(8,128)S(1)} %get-tuple-element.172, f32[2,4,512]{2,1,0:T(4,128)S(1)} %get-tuple-element.170, pred[512,512]{0,1:T(8,128)(4,1)S(1)} %compare_and_fusion), kind=kLoop, calls=%fused_computation.3 | loop fusion | flops 10481664 | bytes 8683520 | tf_op jit(solution)/shard_map/cond/branch_1_fun/while/body/eval_jaxpr/reduce_sum | solution.py:75
  70.6 1.8 conditional.3
  70.6 1.8 copy.54
  72.4 1.9 %divide_convert_fusion = bf16[1,2,4,512,128]{3,4,2,1,0:T(8,128)(2,1)S(1)} fusion(f32[1,2,4,512,128]{3,4,2,1,0:T(8,128)} %get-tuple-element.162, f32[2,4,512]{2,1,0:T(4,128)S(1)} %bitcast.122), kind=kLoop, calls=%fused_computation.48 | loop fusion | flops 1048576 | bytes 3162112 | tf_op jit(solution)/shard_map/convert_element_type | solution.py:109
  74.3 9.5 %convolution_convert_fusion = bf16[512,4096]{1,0:T(8,128)(2,1)} fusion(bf16[512,1024]{0,1:T(8,128)(2,1)S(1)} %bitcast.119, bf16[1024,4096]{1,0:T(8,128)(2,1)} %param.13), kind=kOutput, calls=%fused_computation.47 | convolution fusion | flops 4297064448 | bytes 13631488 | tf_op jit(solution)/shard_map/dot_general | solution.py:112
  83.8 94.0 %reduce-scatter.2.cloned.1.call-done = bf16[128,4096]{1,0:T(8,128)(2,1)} async-done(((bf16[512,4096]{1,0:T(8,128)(2,1)}), bf16[128,4096]{1,0:T(8,128)(2,1)}) %reduce-scatter.2.cloned.1.call-update) | async-done | bytes 1048592 | tf_op jit(solution)/shard_map/reduce_scatter | solution.py:111
  (20 shorter events, 1.9 us)
Async XLA Ops:
  6.5 38.9 %copy-start = (s32[128]{0:T(128)S(1)}, s32[128]{0:T(128)}, u32[]{:S(2)}) copy-start(s32[128]{0:T(128)} %param.12) | copy-start | bytes 1540
  8.3 15.3 %all-to-all-start.1 = ((bf16[128,8,128]{0,2,1:T(8,128)(2,1)}), bf16[128,8,128]{0,2,1:T(8,128)(2,1)S(1)}, u32[]{:S(2)}, u32[]{:S(2)}) async-start(bf16[128,8,128]{0,2,1:T(8,128)(2,1)} %bitcast.33), calls=%async_computation.1 | async-start | bytes 524288 | tf_op jit(solution)/shard_map/all_to_all | solution.py:38
  23.6 10.4 %all-to-all-start.2 = ((bf16[128,8,128]{0,2,1:T(8,128)(2,1)}), bf16[128,8,128]{0,2,1:T(8,128)(2,1)S(1)}, u32[]{:S(2)}, u32[]{:S(2)}) async-start(bf16[128,8,128]{0,2,1:T(8,128)(2,1)} %bitcast.38), calls=%async_computation.2 | async-start | bytes 524288 | tf_op jit(solution)/shard_map/all_to_all | solution.py:39
  34.0 27.6 %all-to-all-start = ((bf16[128,32,128]{2,0,1:T(8,128)(2,1)}), bf16[128,32,128]{2,0,1:T(8,128)(2,1)S(1)}, u32[]{:S(2)}, u32[]{:S(2)}) async-start(bf16[128,32,128]{2,0,1:T(8,128)(2,1)} %copy.35), calls=%async_computation | async-start | bytes 2097152 | tf_op jit(solution)/shard_map/all_to_all | solution.py:37
  37.5 140.3 %reduce-scatter.2.cloned.1.call-start = ((), (), s32[]{:S(2)}) async-start(), calls=%async_computation.4 | async-start | bytes 5242880 | tf_op jit(solution)/shard_map/reduce_scatter | solution.py:111
  39.3 31.3 %collective-permute-start.1 = (bf16[512,2,128]{2,0,1:T(8,128)(2,1)}, bf16[512,2,128]{2,0,1:T(8,128)(2,1)S(1)}, u32[]{:S(2)}, u32[]{:S(2)}) collective-permute-start(bf16[512,2,128]{2,0,1:T(8,128)(2,1)} %bitcast.37), channel_id=1, source_target_pairs={{0,4},{4,8},{8,12},{12,16},{16,20},{20,24},{24,28},{1,5},{5,9},{9,... | collective-permute-start | bytes 786440 | tf_op jit(solution)/shard_map/ppermute | solution.py:13
  40.6 30.0 %collective-permute-start.2 = (bf16[512,2,128]{2,0,1:T(8,128)(2,1)}, bf16[512,2,128]{2,0,1:T(8,128)(2,1)}, u32[]{:S(2)}, u32[]{:S(2)}) collective-permute-start(bf16[512,2,128]{2,0,1:T(8,128)(2,1)} %bitcast.42), channel_id=1, source_target_pairs={{0,4},{4,8},{8,12},{12,16},{16,20},{20,24},{24,28},{1,5},{5,9},{9,... | collective-permute-start | bytes 786440 | tf_op jit(solution)/shard_map/ppermute | solution.py:13
  57.7 2.1 %collective-permute-start = (bf16[512]{0:T(512)(128)(2,1)S(1)}, bf16[512]{0:T(512)(128)(2,1)S(1)}, u32[]{:S(2)}, u32[]{:S(2)}) collective-permute-start(bf16[512]{0:T(512)(128)(2,1)S(1)} %convert_element_type.32), channel_id=1, source_target_pairs={{0,4},{4,8},{8,12},{12,16},{16,20},{20,24},{24,28},{1,5},{5,9},{9,... | collective-permute-start | bytes 3080 | tf_op jit(solution)/shard_map/ppermute | solution.py:13
Sparse Core Ops, SparseCore 0:
  84.0 93.8 reduce-scatter.1
where the time goes:
time: 185 us
  waiting for transfers between devices  106 us (57%)
  starting transfers between devices  20.7 us (11%)
  matrix products  15.9 us (9%)
  between operations  14.8 us (8%)
  blocking collectives  12.3 us (7%)
  local copies, waits for them, and re-layouts  11.3 us (6%)
  other arithmetic  4.25 us (2%)
    reduce_scatter x1, waiting for transfers between devices, body(): lax.psum_scatter(jnp.dot(attn, out_weight, preferred_element_type=jnp.flo...  94 us
    all_gather x1, blocking collectives, body(): query_ids = lax.all_gather(doc_ids, 'uly', axis=0, tiled=True)  12.3 us
    dot_general x1, matrix products, body(): jnp.dot(attn, out_weight, preferred_element_type=jnp.float32)  9.49 us
    ppermute x3, starting transfers between devices, shifted(): lax.ppermute(value, axis, [(source, source + steps) for source in range(f...  7.39 us
    all_to_all x1, waiting for transfers between devices, body(): lax.all_to_all(key_wide, 'uly', split_axis=1, concat_axis=0, tiled=True)  7.13 us
    all_to_all x1, starting transfers between devices, body(): lax.all_to_all(key_wide, 'uly', split_axis=1, concat_axis=0, tiled=True)  6.35 us
    unnamed x5, local copies, waits for them, and re-layouts  5.2 us
    all_to_all x1, waiting for transfers between devices, body(): lax.all_to_all(value_wide, 'uly', split_axis=1, concat_axis=0, tiled=True)  4.06 us
  transfers between devices with their start and end apart: 7, of which 4 were waited for; matrix products, arithmetic and copies ran while one was open for 9% of the time, Pallas kernels for 0%

commit v1 on v0

--- a/solution.py
+++ b/solution.py
@@ -5,6 +5,19 @@
 from jax.sharding import PartitionSpec as P
 
 HEAD_DIM = 128
+
+
+def ring_gather(x, axis, dim):
+    ways = lax.axis_size(axis)
+    up = [(d, (d + 1) % ways) for d in range(ways)]
+    down = [(d, (d - 1) % ways) for d in range(ways)]
+    earlier, later = ([x], [x])
+    for _ in range(ways // 2):
+        earlier.append(lax.ppermute(earlier[-1], axis, up))
+    for _ in range((ways - 1) // 2):
+        later.append(lax.ppermute(later[-1], axis, down))
+    line = jnp.concatenate([*earlier[::-1], *later[1:]], axis=dim)
+    return jnp.roll(line, (lax.axis_index(axis) - ways // 2) * x.shape[dim], axis=dim)
 
 
 def shifted(value, axis, steps):
@@ -28,7 +41,7 @@
     sub_rows = math.gcd(block, 512)
     n_sub = block // sub_rows
     scale = 1.0 / math.sqrt(head_dim)
-    query_ids = lax.all_gather(doc_ids, "uly", axis=0, tiled=True)
+    query_ids = ring_gather(doc_ids, "uly", 0)
     query_split = queries.reshape(rows, heads, head_dim)
     key_wide = jnp.repeat(keys.reshape(rows, kv_heads, head_dim), repeat, axis=1)
     value_wide = jnp.repeat(values.reshape(rows, kv_heads, head_dim), repeat, axis=1)

time: 185 us -> 194 us (1.049)
  waiting for transfers between devices: 106 us -> 119 us
  blocking collectives: 12.3 us -> 0 us
  starting transfers between devices: 20.7 us -> 27.9 us
    ppermute x0 -> x3, waiting for transfers between devices: none -> 16.6 us  [the longest x2 16.6 us: ring_gather(): earlier.append(lax.ppermute(earlier[-1], axis, up))]
    all_gather x1 -> x0, blocking collectives: 12.3 us -> none  [body(): query_ids = lax.all_gather(doc_ids, 'uly', axis=0, tiled=True)]
    ppermute x0 -> x3, starting transfers between devices: none -> 7.16 us  [the longest x2 5.21 us: ring_gather(): earlier.append(lax.ppermute(earlier[-1], axis, up))]
    reduce_scatter x1, waiting for transfers between devices: 94 us -> 90.7 us  [body(): lax.psum_scatter(jnp.dot(attn, out_weight, preferred_element_type=jnp.flo...]
    unnamed x5 -> x12, local copies, waits for them, and re-layouts: 5.2 us -> 5.26 us
  transfers between devices with their start and end apart: 7 -> 10, of which waited for: 4 -> 6; matrix products, arithmetic and copies ran while one was open for 9% -> 9% of each run, Pallas kernels for 0% -> 0%
where the time goes in v1:
time: 194 us; the launch traced here: 193 us
  waiting for transfers between devices  119 us (61%)
  starting transfers between devices  27.9 us (14%)
  matrix products  15.9 us (8%)
  between operations  14.8 us (8%)
  local copies, waits for them, and re-layouts  11.4 us (6%)
  other arithmetic  4.33 us (2%)
    reduce_scatter x1, waiting for transfers between devices, body(): lax.psum_scatter(jnp.dot(attn, out_weight, preferred_element_type=jnp.flo...  90.7 us
    ppermute x2, waiting for transfers between devices, ring_gather(): earlier.append(lax.ppermute(earlier[-1], axis, up))  16.6 us
    dot_general x1, matrix products, body(): jnp.dot(attn, out_weight, preferred_element_type=jnp.float32)  9.5 us
    ppermute x3, starting transfers between devices, shifted(): lax.ppermute(value, axis, [(source, source + steps) for source in range(f...  7.39 us
    all_to_all x1, waiting for transfers between devices, body(): lax.all_to_all(key_wide, 'uly', split_axis=1, concat_axis=0, tiled=True)  7.12 us
    all_to_all x1, starting transfers between devices, body(): lax.all_to_all(key_wide, 'uly', split_axis=1, concat_axis=0, tiled=True)  6.35 us
    unnamed x12, local copies, waits for them, and re-layouts  5.26 us
    ppermute x2, starting transfers between devices, ring_gather(): earlier.append(lax.ppermute(earlier[-1], axis, up))  5.21 us
  transfers between devices with their start and end apart: 10, of which 6 were waited for; matrix products, arithmetic and copies ran while one was open for 9% of the time, Pallas kernels for 0%

profile of v1, /device:TPU:0, one launch (start us, length us, event | category | flops | bytes accessed | tf_op | source)
XLA Modules:
  0.0 193.0 jit_solution(6368680779490408113)
XLA Ops:
  6.5 1.8 copy.38
  8.3 6.3 %all-to-all-start.1 = ((bf16[128,8,128]{0,2,1:T(8,128)(2,1)}), bf16[128,8,128]{0,2,1:T(8,128)(2,1)S(1)}, u32[]{:S(2)}, u32[]{:S(2)}) async-start(bf16[128,8,128]{0,2,1:T(8,128)(2,1)} %bitcast.31), calls=%async_computation.1 | async-start | bytes 524288 | tf_op jit(solution)/shard_map/all_to_all | solution.py:51
  14.7 1.8 copy.41
  16.5 7.1 %all-to-all-done.1 = bf16[128,8,128]{0,2,1:T(8,128)(2,1)S(1)} async-done(((bf16[128,8,128]{0,2,1:T(8,128)(2,1)}), bf16[128,8,128]{0,2,1:T(8,128)(2,1)S(1)}, u32[]{:S(2)}, u32[]{:S(2)}) %all-to-all-start.1) | async-done | bytes 262176 | tf_op jit(solution)/shard_map/all_to_all | solution.py:51
  23.6 3.4 %all-to-all-start.2 = ((bf16[128,8,128]{0,2,1:T(8,128)(2,1)}), bf16[128,8,128]{0,2,1:T(8,128)(2,1)S(1)}, u32[]{:S(2)}, u32[]{:S(2)}) async-start(bf16[128,8,128]{0,2,1:T(8,128)(2,1)} %bitcast.36), calls=%async_computation.2 | async-start | bytes 524288 | tf_op jit(solution)/shard_map/all_to_all | solution.py:52
  27.0 1.6 copy.34
  28.6 1.3 copy.35
  29.9 4.1 %all-to-all-done.2 = bf16[128,8,128]{0,2,1:T(8,128)(2,1)S(1)} async-done(((bf16[128,8,128]{0,2,1:T(8,128)(2,1)}), bf16[128,8,128]{0,2,1:T(8,128)(2,1)S(1)}, u32[]{:S(2)}, u32[]{:S(2)}) %all-to-all-start.2) | async-done | bytes 262176 | tf_op jit(solution)/shard_map/all_to_all | solution.py:52
  34.0 3.5 %all-to-all-start = ((bf16[128,32,128]{2,0,1:T(8,128)(2,1)}), bf16[128,32,128]{2,0,1:T(8,128)(2,1)S(1)}, u32[]{:S(2)}, u32[]{:S(2)}) async-start(bf16[128,32,128]{2,0,1:T(8,128)(2,1)} %copy.35), calls=%async_computation | async-start | bytes 2097152 | tf_op jit(solution)/shard_map/all_to_all | solution.py:50
  37.6 1.9 %collective-permute-start = (s32[128]{0:T(128)S(1)}, s32[128]{0:T(128)S(1)}, u32[]{:S(2)}, u32[]{:S(2)}) collective-permute-start(s32[128]{0:T(128)S(1)} %copy-done), channel_id=1, source_target_pairs={{0,1},{1,2},{2,3},{3,0},{4,5},{5,6},{6,7},{7,4},{8,9},{9,10},{10,1... | collective-permute-start | bytes 1544 | tf_op jit(solution)/shard_map/ppermute | solution.py:16
  39.5 1.9 %collective-permute-start.2 = (s32[128]{0:T(128)S(1)}, s32[128]{0:T(128)S(1)}, u32[]{:S(2)}, u32[]{:S(2)}) collective-permute-start(s32[128]{0:T(128)S(1)} %copy-done), channel_id=1, source_target_pairs={{0,3},{1,0},{2,1},{3,2},{4,7},{5,4},{6,5},{7,6},{8,11},{9,8},{10,9... | collective-permute-start | bytes 1544 | tf_op jit(solution)/shard_map/ppermute | solution.py:18
  41.5 14.5 %collective-permute-done = s32[128]{0:T(128)S(1)} collective-permute-done((s32[128]{0:T(128)S(1)}, s32[128]{0:T(128)S(1)}, u32[]{:S(2)}, u32[]{:S(2)}) %collective-permute-start) | collective-permute-done | bytes 544 | tf_op jit(solution)/shard_map/ppermute | solution.py:16
  56.0 3.3 %collective-permute-start.1 = (s32[128]{0:T(128)S(1)}, s32[128]{0:T(128)S(1)}, u32[]{:S(2)}, u32[]{:S(2)}) collective-permute-start(s32[128]{0:T(128)S(1)} %collective-permute-done), channel_id=1, source_target_pairs={{0,1},{1,2},{2,3},{3,0},{4,5},{5,6},{6,7},{7,4},{8,9},{9,10},{10,1... | collective-permute-start | bytes 1544 | tf_op jit(solution)/shard_map/ppermute | solution.py:16
  59.3 2.1 %collective-permute-done.1 = s32[128]{0:T(128)S(1)} collective-permute-done((s32[128]{0:T(128)S(1)}, s32[128]{0:T(128)S(1)}, u32[]{:S(2)}, u32[]{:S(2)}) %collective-permute-start.1) | collective-permute-done | bytes 544 | tf_op jit(solution)/shard_map/ppermute | solution.py:16
  64.5 4.8 %collective-permute-start.5 = (bf16[512,2,128]{2,0,1:T(8,128)(2,1)}, bf16[512,2,128]{2,0,1:T(8,128)(2,1)}, u32[]{:S(2)}, u32[]{:S(2)}) collective-permute-start(bf16[512,2,128]{2,0,1:T(8,128)(2,1)} %bitcast.40), channel_id=1, source_target_pairs={{0,4},{4,8},{8,12},{12,16},{16,20},{20,24},{24,28},{1,5},{5,9},{9,... | collective-permute-start | bytes 786440 | tf_op jit(solution)/shard_map/ppermute | solution.py:26
  73.3 8.8 %conditional.2 = (f32[1,2,4,512,128]{4,3,2,1,0:T(8,128)S(1)}, f32[1,2,4,512]{3,2,1,0:T(4,128)S(1)}, f32[1,2,4,512]{3,2,1,0:T(4,128)S(1)}) conditional(s32[]{:T(128)} %convert_element_type.35, () %tuple.24, (s32[]{:T(128)}, s32[512]{0:T(512)S(1)}, s32[1,512]{1,0:T(1,128)S(1)}, s32[512]{0:T(512)S(1)}, s32[1,512]{1,0:T(1,128)S(1)}, ...), branch_computations={%region_0.1_spmd, %region_1.4_spmd} | conditional | flops 1102336512 | bytes 30093364 | solution.py:104
  73.7 2.5 %fusion = (f32[2,4,512]{2,1,0:T(4,128)S(1)}, f32[2,512,512,4]{2,1,3,0:T(8,128)S(1)}) fusion(pred[512,512]{0,1:T(8,128)(4,1)S(1)} %compare_and_fusion, bf16[1,512,2,4,128]{4,1,3,2,0:T(8,128)(2,1)S(1)} %get-tuple-element.136, bf16[512,2,128]{2,0,1:T(8,128)(2,1)} %get-tuple-element.134), kind=kOutput, calls=%fused_computation.2 | convolution fusion | flops 543158272 | bytes 9977856 | tf_op jit(solution)/shard_map/cond/branch_1_fun/while/body/eval_jaxpr/qkgd,pkd->kgqp/dot_general | solution.py:76
  76.2 3.9 %add_bitcast_fusion = f32[1,2,4,512,128]{4,3,2,1,0:T(8,128)S(1)} fusion(f32[2,512,512,4]{2,1,3,0:T(8,128)S(1)} %get-tuple-element.174, f32[2,4,512]{2,1,0:T(4,128)S(1)} %get-tuple-element.172, pred[512,512]{0,1:T(8,128)(4,1)S(1)} %compare_and_fusion, f32[2,4,512]{2,1,0:T(4,128)S(1)} %get-tuple-element.171, bf16[512,2,128]{2,0,1:T(8,128)(2,1)} %get-tuple-element.138), kind=kOutput, calls=%fused_computation.7 | convolution fusion | flops 547880960 | bytes 11042816 | tf_op jit(solution)/shard_map/cond/branch_1_fun/while/body/eval_jaxpr/kgqp,pkd->kgqd/dot_general | solution.py:89
  80.1 2.0 %fusion.1 = f32[2,4,512]{2,1,0:T(4,128)S(1)} fusion(f32[2,512,512,4]{2,1,3,0:T(8,128)S(1)} %get-tuple-element.174, f32[2,4,512]{2,1,0:T(4,128)S(1)} %get-tuple-element.172, pred[512,512]{0,1:T(8,128)(4,1)S(1)} %compare_and_fusion), kind=kLoop, calls=%fused_computation.3 | loop fusion | flops 10481664 | bytes 8683520 | tf_op jit(solution)/shard_map/cond/branch_1_fun/while/body/eval_jaxpr/reduce_sum | solution.py:88
  82.2 1.9 conditional.3
  82.2 1.8 copy.54
  84.0 1.9 divide_convert_fusion
  85.9 9.5 %convolution_convert_fusion = bf16[512,4096]{1,0:T(8,128)(2,1)} fusion(bf16[512,1024]{0,1:T(8,128)(2,1)S(1)} %bitcast.117, bf16[1024,4096]{1,0:T(8,128)(2,1)} %param.13), kind=kOutput, calls=%fused_computation.47 | convolution fusion | flops 4297064448 | bytes 13631488 | tf_op jit(solution)/shard_map/dot_general | solution.py:125
  95.5 90.7 %reduce-scatter.2.cloned.1.call-done = bf16[128,4096]{1,0:T(8,128)(2,1)} async-done(((bf16[512,4096]{1,0:T(8,128)(2,1)}), bf16[128,4096]{1,0:T(8,128)(2,1)}) %reduce-scatter.2.cloned.1.call-update) | async-done | bytes 1048592 | tf_op jit(solution)/shard_map/reduce_scatter | solution.py:124
  (34 shorter events, 6.3 us)
Async XLA Ops:
  6.5 31.1 %copy-start = (s32[128]{0:T(128)S(1)}, s32[128]{0:T(128)}, u32[]{:S(2)}) copy-start(s32[128]{0:T(128)} %param.12) | copy-start | bytes 1540
  8.3 15.3 %all-to-all-start.1 = ((bf16[128,8,128]{0,2,1:T(8,128)(2,1)}), bf16[128,8,128]{0,2,1:T(8,128)(2,1)S(1)}, u32[]{:S(2)}, u32[]{:S(2)}) async-start(bf16[128,8,128]{0,2,1:T(8,128)(2,1)} %bitcast.31), calls=%async_computation.1 | async-start | bytes 524288 | tf_op jit(solution)/shard_map/all_to_all | solution.py:51
  23.6 10.4 %all-to-all-start.2 = ((bf16[128,8,128]{0,2,1:T(8,128)(2,1)}), bf16[128,8,128]{0,2,1:T(8,128)(2,1)S(1)}, u32[]{:S(2)}, u32[]{:S(2)}) async-start(bf16[128,8,128]{0,2,1:T(8,128)(2,1)} %bitcast.36), calls=%async_computation.2 | async-start | bytes 524288 | tf_op jit(solution)/shard_map/all_to_all | solution.py:52
  34.0 39.2 %all-to-all-start = ((bf16[128,32,128]{2,0,1:T(8,128)(2,1)}), bf16[128,32,128]{2,0,1:T(8,128)(2,1)S(1)}, u32[]{:S(2)}, u32[]{:S(2)}) async-start(bf16[128,32,128]{2,0,1:T(8,128)(2,1)} %copy.35), calls=%async_computation | async-start | bytes 2097152 | tf_op jit(solution)/shard_map/all_to_all | solution.py:50
  37.5 148.6 %reduce-scatter.2.cloned.1.call-start = ((), (), s32[]{:S(2)}) async-start(), calls=%async_computation.4 | async-start | bytes 5242880 | tf_op jit(solution)/shard_map/reduce_scatter | solution.py:124
  37.6 18.4 %collective-permute-start = (s32[128]{0:T(128)S(1)}, s32[128]{0:T(128)S(1)}, u32[]{:S(2)}, u32[]{:S(2)}) collective-permute-start(s32[128]{0:T(128)S(1)} %copy-done), channel_id=1, source_target_pairs={{0,1},{1,2},{2,3},{3,0},{4,5},{5,6},{6,7},{7,4},{8,9},{9,10},{10,1... | collective-permute-start | bytes 1544 | tf_op jit(solution)/shard_map/ppermute | solution.py:16
  39.5 21.9 %collective-permute-start.2 = (s32[128]{0:T(128)S(1)}, s32[128]{0:T(128)S(1)}, u32[]{:S(2)}, u32[]{:S(2)}) collective-permute-start(s32[128]{0:T(128)S(1)} %copy-done), channel_id=1, source_target_pairs={{0,3},{1,0},{2,1},{3,2},{4,7},{5,4},{6,5},{7,6},{8,11},{9,8},{10,9... | collective-permute-start | bytes 1544 | tf_op jit(solution)/shard_map/ppermute | solution.py:18
  56.0 5.4 %collective-permute-start.1 = (s32[128]{0:T(128)S(1)}, s32[128]{0:T(128)S(1)}, u32[]{:S(2)}, u32[]{:S(2)}) collective-permute-start(s32[128]{0:T(128)S(1)} %collective-permute-done), channel_id=1, source_target_pairs={{0,1},{1,2},{2,3},{3,0},{4,5},{5,6},{6,7},{7,4},{8,9},{9,10},{10,1... | collective-permute-start | bytes 1544 | tf_op jit(solution)/shard_map/ppermute | solution.py:16
  63.2 19.0 %collective-permute-start.4 = (bf16[512,2,128]{2,0,1:T(8,128)(2,1)}, bf16[512,2,128]{2,0,1:T(8,128)(2,1)S(1)}, u32[]{:S(2)}, u32[]{:S(2)}) collective-permute-start(bf16[512,2,128]{2,0,1:T(8,128)(2,1)} %bitcast.35), channel_id=1, source_target_pairs={{0,4},{4,8},{8,12},{12,16},{16,20},{20,24},{24,28},{1,5},{5,9},{9,... | collective-permute-start | bytes 786440 | tf_op jit(solution)/shard_map/ppermute | solution.py:26
  64.5 17.7 %collective-permute-start.5 = (bf16[512,2,128]{2,0,1:T(8,128)(2,1)}, bf16[512,2,128]{2,0,1:T(8,128)(2,1)}, u32[]{:S(2)}, u32[]{:S(2)}) collective-permute-start(bf16[512,2,128]{2,0,1:T(8,128)(2,1)} %bitcast.40), channel_id=1, source_target_pairs={{0,4},{4,8},{8,12},{12,16},{16,20},{20,24},{24,28},{1,5},{5,9},{9,... | collective-permute-start | bytes 786440 | tf_op jit(solution)/shard_map/ppermute | solution.py:26
  69.4 2.1 %collective-permute-start.3 = (bf16[512]{0:T(512)(128)(2,1)S(1)}, bf16[512]{0:T(512)(128)(2,1)S(1)}, u32[]{:S(2)}, u32[]{:S(2)}) collective-permute-start(bf16[512]{0:T(512)(128)(2,1)S(1)} %get-tuple-element.165), channel_id=1, source_target_pairs={{0,4},{4,8},{8,12},{12,16},{16,20},{20,24},{24,28},{1,5},{5,9},{9,... | collective-permute-start | bytes 3080 | tf_op jit(solution)/shard_map/ppermute | solution.py:26
Sparse Core Ops, SparseCore 0:
  95.6 90.5 reduce-scatter.1
